TPU v7x, 32 devices: a whole 2x2x4 slice. The times are simulated.
32 devices in a mesh: fsdp: 16 (over z, y, x), mat: 2 (over core).
Axes of the slice: x: 2, y: 2, z: 4, core: 2. Of those that a mesh axis runs over, the one named last changes fastest.
Arguments:
- momentum: float32 [8192, 4096], P(('mat', 'fsdp')), parts along dimension 0, may hold values from -6 to 6
- grad: bfloat16 [8192, 4096], P(('mat', 'fsdp')), parts along dimension 0, may hold values from -6 to 6
- q_basis: float32 [8192, 512], P(('mat', 'fsdp')), parts along dimension 0, may hold values from -6 to 6
Outputs:
- momentum_next: float32 [8192, 4096], P(('mat', 'fsdp')), parts along dimension 0
- update: bfloat16 [8192, 4096], P(('mat', 'fsdp')), parts along dimension 0
- q_next: float32 [8192, 512], P(('mat', 'fsdp')), parts along dimension 0
There are 2 independent parts, one for each index of `mat`. A program takes and returns all parts, laid end to end along the dimension named above; each array names one. Nothing has to cross between parts.
All inputs are finite; a program needn't handle non-finite values.
Results may differ from a plain program's by a relative error of at most 0.0076.
Values may be sent and summed in bfloat16 or wider, within the bound.
A program may use at most 128 MiB of HBM per device.

v0:
```python
import math

import jax
import jax.numpy as jnp
from jax import lax
from jax.sharding import PartitionSpec as P

damping = 0.95
epsilon = 1e-06


def lower_inverse(gram_total):
    order_size = gram_total.shape[0]
    identity = jnp.eye(order_size, dtype=jnp.float32)
    ridge_term = 0.0001 * jnp.trace(gram_total) / order_size
    factor_lower = jnp.linalg.cholesky(gram_total + ridge_term * identity)
    return lax.linalg.triangular_solve(factor_lower, identity, left_side=True, lower=True)


def per_device(momentum, grad, q_basis):
    own_rows = momentum.shape[0]
    basis_rows = q_basis.shape[0]
    devices = lax.axis_size("fsdp")
    features = basis_rows * devices
    blended = momentum + grad.astype(jnp.float32)
    blended_low = blended.astype(jnp.bfloat16)
    basis_low = q_basis.astype(jnp.bfloat16)
    projected = jnp.dot(
        blended_low,
        lax.all_gather(basis_low, "fsdp", axis=0, tiled=True),
        preferred_element_type=jnp.float32,
    )
    local_gram = jnp.dot(projected.T, projected, precision=lax.Precision.HIGHEST)
    partial_sum = jnp.dot(blended.T, projected, precision=lax.Precision.HIGHEST)
    summed, gram_total = lax.psum((partial_sum, local_gram), "fsdp")
    inverse = lower_inverse(gram_total)
    summed = jnp.dot(summed, inverse.T, precision=lax.Precision.HIGHEST)
    orthonormal = jnp.dot(projected, inverse.T, precision=lax.Precision.HIGHEST)
    column_rms = jnp.sqrt(jnp.mean(summed * summed, axis=0) + epsilon)
    q_full = summed / column_rms
    q_next = lax.dynamic_slice_in_dim(q_full, lax.axis_index("fsdp") * basis_rows, basis_rows, 0)
    q_low = q_full.astype(jnp.bfloat16)
    stacked = jnp.concatenate(
        [(orthonormal * column_rms).astype(jnp.bfloat16), orthonormal.astype(jnp.bfloat16)], axis=0
    )
    result = jnp.dot(stacked, q_low.T, preferred_element_type=jnp.float32)
    total_rows = own_rows * devices
    momentum_next = blended - (1.0 - damping) * result[:own_rows]
    update = (math.sqrt(total_rows * features / q_basis.shape[1]) * result[own_rows:]).astype(
        jnp.bfloat16
    )
    return (momentum_next, update, q_next)


def solution(mesh):
    in_specs = (P(("mat", "fsdp"), None), P(("mat", "fsdp"), None), P(("mat", "fsdp"), None))
    out_specs = (P(("mat", "fsdp"), None), P(("mat", "fsdp"), None), P(("mat", "fsdp"), None))
    return jax.shard_map(
        per_device, mesh=mesh, in_specs=in_specs, out_specs=out_specs, check_vma=False
    )
```

profile of v0, /device:TPU:0, one launch (start us, length us, event | category | flops | bytes accessed | tf_op | source)
XLA Modules:
  0.0 581.3 jit_solution(14707892405092458225)
XLA Ops:
  7.2 1.8 convert_element_type.30
  9.1 80.6 %all-gather.2.cloned.1.call-done = bf16[4096,512]{1,0:T(8,128)(2,1)} async-done(((bf16[256,512]{1,0:T(8,128)(2,1)}), bf16[4096,512]{1,0:T(8,128)(2,1)}) %all-gather.2.cloned.1.call-update) | async-done | bytes 4194320 | tf_op jit(solution)/shard_map/all_gather | solution.py:30
  89.7 5.4 fusion.4
  95.1 2.0 fusion.47
  97.1 9.5 %fusion.6 = f32[4096,512]{1,0:T(8,128)} fusion(f32[256,512]{1,0:T(8,128)S(1)} %fusion.4, f32[256,4096]{1,0:T(8,128)S(1)} %copy-done, bf16[256,4096]{1,0:T(8,128)(2,1)S(1)} %copy-done.2), kind=kOutput, calls=%fused_computation.13 | convolution fusion | flops 6444548096 | bytes 15204352 | tf_op jit(solution)/shard_map/dot_general | solution.py:34
  106.7 1.1 fusion.8
  107.8 276.2 %all-reduce.4.cloned.1.call-done = (f32[4096,512]{1,0:T(8,128)}, f32[512,512]{0,1:T(8,128)}) async-done(((f32[4096,512]{1,0:T(8,128)}, f32[512,512]{0,1:T(8,128)}), (f32[4096,512]{1,0:T(8,128)}, f32[512,512]{0,1:T(8,128)})) %all-reduce.4.cloned.1.call-update) | async-done | bytes 9437200 | tf_op jit(solution)/shard_map/psum | solution.py:35
  384.0 2.0 select_reduce_fusion
  386.6 1.3 select_add_fusion
  388.0 1.3 copy.7
  389.3 1.4 fusion.7
  390.8 11.7 %cholesky.103 = f32[128,128]{1,0:T(8,128)S(1)} custom-call(f32[128,128]{1,0:T(8,128)S(1)} %cholesky.263), custom_call_target="Cholesky" | custom-call | tf_op jit(solution)/shard_map/jit(cholesky)/cholesky | solution.py:16
  402.6 9.8 %custom-call.30 = f32[1,128,128]{1,2,0:T(8,128)S(1)} custom-call(f32[1,128,128]{2,1,0:T(8,128)S(1)} %get-tuple-element.36), custom_call_target="InvertDiagBlocksLowerTriangular" | custom-call | tf_op jit(solution)/shard_map/jit(cholesky)/cholesky | solution.py:16
  413.2 11.7 %cholesky.215 = f32[128,128]{1,0:T(8,128)S(1)} custom-call(f32[128,128]{1,0:T(8,128)S(1)} %cholesky.267), custom_call_target="Cholesky" | custom-call | tf_op jit(solution)/shard_map/jit(cholesky)/cholesky | solution.py:16
  425.1 10.0 %custom-call.31 = f32[1,128,128]{1,2,0:T(8,128)S(1)} custom-call(f32[1,128,128]{2,1,0:T(8,128)S(1)} %get-tuple-element.34), custom_call_target="InvertDiagBlocksLowerTriangular" | custom-call | tf_op jit(solution)/shard_map/jit(cholesky)/cholesky | solution.py:16
  435.5 1.5 convolution_subtract_fusion.4
  437.1 11.7 %cholesky.236 = f32[128,128]{1,0:T(8,128)S(1)} custom-call(f32[128,128]{1,0:T(8,128)S(1)} %cholesky.272), custom_call_target="Cholesky" | custom-call | tf_op jit(solution)/shard_map/jit(cholesky)/cholesky | solution.py:16
  448.9 9.8 %custom-call.32 = f32[1,128,128]{1,2,0:T(8,128)S(1)} custom-call(f32[1,128,128]{2,1,0:T(8,128)S(1)} %get-tuple-element.32), custom_call_target="InvertDiagBlocksLowerTriangular" | custom-call | tf_op jit(solution)/shard_map/jit(cholesky)/cholesky | solution.py:16
  459.0 1.3 convolution_subtract_fusion.5
  460.4 11.9 %cholesky.253 = f32[128,128]{1,0:T(8,128)S(1)} custom-call(f32[128,128]{1,0:T(8,128)S(1)} %convolution_subtract_fusion.5), custom_call_target="Cholesky" | custom-call | tf_op jit(solution)/shard_map/jit(cholesky)/cholesky | solution.py:16
  472.4 0.6 compare_reduce_fusion.1
  473.0 0.6 compare_reduce_fusion
  473.7 0.6 compare_reduce_fusion.2
  476.8 1.1 select_select_fusion
  477.9 14.1 %while.1 = (s32[]{:T(128)}, f32[512,512]{0,1:T(8,128)}, s32[4,2]{0,1:T(2,128)S(1)}, f32[4,128,128]{2,1,0:T(8,128)}, s32[]{:T(128)}) while((s32[]{:T(128)}, f32[512,512]{0,1:T(8,128)}, s32[4,2]{0,1:T(2,128)S(1)}, f32[4,128,128]{2,1,0:T(8,128)}, s32[]{:T(128)}) %tuple.33), condition=%wide.while_cond, body=%wide.while_body.sunk | while | flops 2 | bytes 393329 | solution.py:17
  477.9 0.5 fusion.60
  478.5 2.2 dynamic-slice.7
  480.8 0.6 bitcast_dynamic-update-slice_fusion.2
  481.5 0.5 fusion.60
  482.0 2.2 dynamic-slice.7
  484.3 0.6 bitcast_dynamic-update-slice_fusion.2
  485.0 0.5 fusion.60
  485.5 2.2 dynamic-slice.7
  487.8 0.6 bitcast_dynamic-update-slice_fusion.2
  488.5 0.5 fusion.60
  489.1 2.1 dynamic-slice.7
  491.3 0.6 bitcast_dynamic-update-slice_fusion.2
  491.9 40.1 %custom-call.33 = f32[4,128,128]{1,2,0:T(8,128)S(1)} custom-call(f32[4,128,128]{2,1,0:T(8,128)} %get-tuple-element.10), custom_call_target="InvertDiagBlocksLowerTriangular" | custom-call | tf_op jit(solution)/shard_map/triangular_solve | solution.py:17
  532.4 1.4 convolution_subtract_fusion.1
  533.8 0.4 fusion.35
  534.3 1.9 convolution_subtract_fusion
  536.6 2.4 convolution_subtract_fusion.2
  539.5 17.4 %multiply_reduce_fusion = (f32[512]{0:T(512)S(1)}, f32[4096,512]{1,0:T(8,128)S(1)}) fusion(f32[4096,512]{1,0:T(8,128)} %get-tuple-element.23, f32[128,512]{1,0:T(8,128)S(1)} %fusion.32, f32[128,512]{1,0:T(8,128)S(1)} %fusion.33, f32[128,512]{1,0:T(8,128)S(1)} %fusion.35, f32[128,512]{1,0:T(8,128)S(1)} %fusion.23), kind=kOutput, calls=%fused_computation.2 | convolution fusion | flops 12889882624 | bytes 17827840 | tf_op jit(solution)/shard_map/dot_general | solution.py:37
  556.9 1.1 multiply_convert_fusion
  558.0 1.1 broadcast_divide_fusion
  559.0 0.8 constant_dynamic-slice_fusion.1
  559.9 5.6 fusion.2
  565.5 8.4 %fusion = (bf16[256,4096]{1,0:T(8,128)(2,1)}, f32[256,4096]{1,0:T(8,128)}) fusion(f32[512,4096]{1,0:T(8,128)} %fusion.2, f32[256,4096]{1,0:T(8,128)S(1)} %copy-done.1, bf16[256,4096]{1,0:T(8,128)(2,1)} %param.4), kind=kLoop, calls=%fused_computation.4 | loop fusion | flops 6291456 | bytes 20971520 | tf_op jit(solution)/shard_map/convert_element_type | solution.py:49
  (53 shorter events, 4.1 us)
Async XLA Ops:
  7.2 82.5 %all-gather.2.cloned.1.call-start = ((), (), s32[]{:S(2)}) async-start(), calls=%async_computation | async-start | bytes 4456448 | tf_op jit(solution)/shard_map/all_gather | solution.py:30
  9.0 88.1 %copy-start.2 = (bf16[256,4096]{1,0:T(8,128)(2,1)S(1)}, bf16[256,4096]{1,0:T(8,128)(2,1)}, u32[]{:S(2)}) copy-start(bf16[256,4096]{1,0:T(8,128)(2,1)} %param.4) | copy-start | bytes 6291460
  9.0 374.9 %all-reduce.4.cloned.1.call-start = ((), (), s32[]{:S(2)}) async-start(), calls=%async_computation.1 | async-start | bytes 18874368 | tf_op jit(solution)/shard_map/psum | solution.py:35
  89.7 7.5 %copy-start = (f32[256,4096]{1,0:T(8,128)S(1)}, f32[256,4096]{1,0:T(8,128)}, u32[]{:S(2)}) copy-start(f32[256,4096]{1,0:T(8,128)} %param.3) | copy-start | bytes 12582916
  384.0 5.3 copy-start.3
  390.7 34.4 %copy-start.5 = (f32[512,512]{1,0:T(8,128)}, f32[512,512]{1,0:T(8,128)S(1)}, u32[]{:S(2)}) copy-start(f32[512,512]{1,0:T(8,128)S(1)} %fusion.7) | copy-start | bytes 3145732
  435.0 97.4 %copy-start.4 = (f32[512,512]{0,1:T(8,128)S(1)}, f32[512,512]{0,1:T(8,128)}, u32[]{:S(2)}) copy-start(f32[512,512]{0,1:T(8,128)} %fusion.8) | copy-start | bytes 3145732
  559.9 5.7 copy-start.1
Sparse Core Ops, SparseCore 0:
  11.3 78.3 all-gather.1
  106.7 277.1 all-reduce.3
where the time goes:
time: 586 us; the launch traced here: 581 us
  waiting for transfers between devices  357 us (61%)
  other arithmetic  137 us (23%)
  matrix products  52.4 us (9%)
  between operations  18 us (3%)
  local copies, waits for them, and re-layouts  16.9 us (3%)
    psum x1, waiting for transfers between devices, per_device(): summed, gram_total = lax.psum((partial_sum, local_gram), 'fsdp')  276 us
    all_gather x1, waiting for transfers between devices, per_device(): lax.all_gather(basis_low, 'fsdp', axis=0, tiled=True)  80.6 us
    another operation x14, other arithmetic, lower_inverse(): factor_lower = jnp.linalg.cholesky(gram_total + ridge_term * identity)  78.7 us
    another operation x3, other arithmetic, lower_inverse(): lax.linalg.triangular_solve(factor_lower, identity, left_side=True, lower...  41.2 us
    dot_general x1, matrix products, per_device(): summed = jnp.dot(summed, inverse.T, precision=lax.Precision.HIGHEST)  17.4 us
    another operation x20, local copies, waits for them, and re-layouts  14 us
  transfers between devices with their start and end apart: 2, of which 2 were waited for; matrix products, arithmetic and copies ran while one was open for 0% of the time, Pallas kernels for 0%

commit v1 on v0

v1 whole, which is shorter than its diff:
```python
import functools
import math

import jax
import jax.numpy as jnp
from jax import lax
from jax.experimental import pallas as pl
from jax.experimental.pallas import tpu as pltpu
from jax.sharding import PartitionSpec as P

damping = 0.95
epsilon = 1e-06
HIGHEST = lax.Precision.HIGHEST
MESH = pl.DeviceIdType.MESH


def grid_of(mesh):
    n = mesh.shape["fsdp"]
    at = list(mesh.axis_names).index("fsdp")
    try:
        line = mesh.devices.swapaxes(0, at).reshape(n, -1)[:, 0]
        spots = [tuple(d.coords) for d in line]
        axes = []
        for d in range(3):
            size = len({s[d] for s in spots})
            if size > 1:
                stride = next(i for i in range(n) if spots[i][d] != spots[0][d])
                axes.append((stride, size))
        sizes = [size for _, size in sorted(axes, reverse=True)]
        if math.prod(sizes) == n:
            return tuple([1] * (3 - len(sizes)) + sizes)
    except AttributeError:
        pass
    return (n // 4, 2, 2) if n % 4 == 0 else (1, 1, n)


def cut(rows, unit, sizes):
    units = rows // unit
    side = (units * 3 + 4) // 8
    counts = [side, side, units - 2 * side]
    long_axis = max(range(3), key=lambda d: sizes[d])
    others = [d for d in range(3) if d != long_axis]
    orders = [
        (long_axis, others[0], others[1]),
        (others[1], long_axis, others[0]),
        (others[0], others[1], long_axis),
    ]
    pieces, start = [], 0
    for count, order in zip(counts, orders):
        if count:
            pieces.append((start, count * unit, order))
        start += count * unit
    return pieces


def position(sizes):
    me = lax.axis_index("fsdp")
    return [
        lax.div(me, sizes[1] * sizes[2]),
        lax.rem(lax.div(me, sizes[2]), sizes[1]),
        lax.rem(me, sizes[2]),
    ]


def shifted(mine, sizes, d, off):
    return lax.rem(mine[d] + off, sizes[d])


def device_at(mine, sizes, d, coordinate):
    spot = list(mine)
    spot[d] = coordinate
    return {"fsdp": (spot[0] * sizes[1] + spot[1]) * sizes[2] + spot[2]}


def greet(mine, sizes):
    barrier = pltpu.get_barrier_semaphore()
    for d in range(3):
        for off in range(1, sizes[d]):
            target = device_at(mine, sizes, d, shifted(mine, sizes, d, off))
            pl.semaphore_signal(barrier, inc=1, device_id=target, device_id_type=MESH)
    pl.semaphore_wait(barrier, sum(sizes) - 3)


def gather_kernel(sizes, pieces, x_ref, o_ref, own_sem, send_sem, recv_sem):
    mine = position(sizes)
    own = pltpu.make_async_copy(x_ref, o_ref.at[mine[0], mine[1], mine[2]], own_sem)
    own.start()
    greet(mine, sizes)

    def block(piece, phase, coordinate):
        start, rows, order = piece
        index = list(mine)
        index[order[phase]] = coordinate
        for d in order[:phase]:
            index[d] = slice(None)
        return o_ref.at[index[0], index[1], index[2], pl.ds(start, rows)]

    sent = []
    for phase in range(3):
        if phase == 1:
            own.wait()
        for p, piece in enumerate(pieces):
            if phase:
                d = piece[2][phase - 1]
                for off in range(1, sizes[d]):
                    landed = block(piece, phase - 1, shifted(mine, sizes, d, sizes[d] - off))
                    pltpu.make_async_copy(landed, landed, recv_sem.at[p, phase - 1, off]).wait()
            d = piece[2][phase]
            for off in range(1, sizes[d]):
                target = block(piece, phase, mine[d])
                source = x_ref.at[pl.ds(piece[0], piece[1])] if phase == 0 else target
                copy = pltpu.make_async_remote_copy(
                    src_ref=source,
                    dst_ref=target,
                    send_sem=send_sem.at[p, phase, off],
                    recv_sem=recv_sem.at[p, phase, off],
                    device_id=device_at(mine, sizes, d, shifted(mine, sizes, d, off)),
                    device_id_type=MESH,
                )
                copy.start()
                sent.append(copy)
    for p, piece in enumerate(pieces):
        d = piece[2][2]
        for off in range(1, sizes[d]):
            landed = block(piece, 2, shifted(mine, sizes, d, sizes[d] - off))
            pltpu.make_async_copy(landed, landed, recv_sem.at[p, 2, off]).wait()
    for copy in sent:
        copy.wait_send()


def gather(x, sizes, number):
    rows, columns = x.shape
    unit = 8 if x.dtype == jnp.float32 else 16
    pieces = cut(rows, unit, sizes)
    sems = pltpu.SemaphoreType.DMA((len(pieces), 3, max(sizes)))
    out = pl.pallas_call(
        functools.partial(gather_kernel, sizes, pieces),
        out_shape=jax.ShapeDtypeStruct(sizes + (rows, columns), x.dtype),
        in_specs=[pl.BlockSpec(memory_space=pltpu.VMEM)],
        out_specs=pl.BlockSpec(memory_space=pltpu.VMEM),
        scratch_shapes=[pltpu.SemaphoreType.DMA, sems, sems],
        compiler_params=pltpu.CompilerParams(
            collective_id=number, has_side_effects=True, vmem_limit_bytes=32 * 2**20
        ),
        name=f"gather_{number}",
    )(x)
    return out.reshape(math.prod(sizes) * rows, columns)


def reduce_kernel(sizes, pieces, x_ref, o_ref, *scratch):
    mine = position(sizes)
    count = len(pieces)
    landing = scratch[: 3 * count]
    sums = scratch[3 * count : 5 * count]
    send_sem, recv_sem = scratch[5 * count :]
    greet(mine, sizes)
    sent = []

    def send(p, phase, d, off, source):
        copy = pltpu.make_async_remote_copy(
            src_ref=source,
            dst_ref=landing[3 * p + phase].at[off - 1],
            send_sem=send_sem.at[p, phase, off],
            recv_sem=recv_sem.at[p, phase, off],
            device_id=device_at(mine, sizes, d, shifted(mine, sizes, d, off)),
            device_id_type=MESH,
        )
        copy.start()
        sent.append(copy)

    def arrive(p, phase, d):
        for off in range(1, sizes[d]):
            here = landing[3 * p + phase].at[off - 1]
            pltpu.make_async_copy(here, here, recv_sem.at[p, phase, off]).wait()

    for p, (start, rows, order) in enumerate(pieces):
        d = order[2]
        for off in range(1, sizes[d]):
            index = [slice(None)] * 3
            index[d] = shifted(mine, sizes, d, off)
            send(p, 0, d, off, x_ref.at[index[0], index[1], index[2], pl.ds(start, rows)])

    for p, (start, rows, order) in enumerate(pieces):
        a, b, c = order
        arrive(p, 0, c)
        low, high = min(a, b), max(a, b)
        for off in list(range(1, sizes[b])) + [0]:
            at_b = shifted(mine, sizes, b, off)

            def one(at_a, _, off=off, at_b=at_b):
                index = [None] * 3
                index[a], index[b], index[c] = at_a, at_b, mine[c]
                total = x_ref[index[0], index[1], index[2], pl.ds(start, rows)].astype(jnp.float32)
                for k in range(sizes[c] - 1):
                    total += landing[3 * p][k, index[low], index[high]].astype(jnp.float32)
                if off:
                    sums[2 * p][off - 1, at_a] = total.astype(x_ref.dtype)
                else:
                    sums[2 * p + 1][at_a] = total
                return 0

            lax.fori_loop(0, sizes[a], one, 0)
        for off in range(1, sizes[b]):
            send(p, 1, b, off, sums[2 * p].at[off - 1])

    for p, (start, rows, order) in enumerate(pieces):
        a, b, c = order
        arrive(p, 1, b)
        for off in list(range(1, sizes[a])) + [0]:
            at_a = shifted(mine, sizes, a, off)
            total = sums[2 * p + 1][at_a]
            for k in range(sizes[b] - 1):
                total += landing[3 * p + 1][k, at_a].astype(jnp.float32)
            if off:
                landing[3 * p + 2][sizes[a] - 1 + off - 1] = total.astype(x_ref.dtype)
            else:
                sums[2 * p + 1][at_a] = total
        for off in range(1, sizes[a]):
            send(p, 2, a, off, landing[3 * p + 2].at[sizes[a] - 1 + off - 1])

    for p, (start, rows, order) in enumerate(pieces):
        a = order[0]
        arrive(p, 2, a)
        total = sums[2 * p + 1][mine[a]]
        for k in range(sizes[a] - 1):
            total += landing[3 * p + 2][k].astype(jnp.float32)
        o_ref[pl.ds(start, rows)] = total
    for copy in sent:
        copy.wait_send()


def reduce_scatter(x, sizes, number):
    n = math.prod(sizes)
    rows, columns = x.shape[0] // n, x.shape[1]
    unit = 8 if x.dtype == jnp.float32 else 16
    pieces = cut(rows, unit, sizes)
    landing, sums = [], []
    for _, part, (a, b, c) in pieces:
        low, high = min(a, b), max(a, b)
        many = lambda k: max(k, 1)
        landing += [
            pltpu.VMEM((many(sizes[c] - 1), sizes[low], sizes[high], part, columns), x.dtype),
            pltpu.VMEM((many(sizes[b] - 1), sizes[a], part, columns), x.dtype),
            pltpu.VMEM((many(2 * (sizes[a] - 1)), part, columns), x.dtype),
        ]
        sums += [
            pltpu.VMEM((many(sizes[b] - 1), sizes[a], part, columns), x.dtype),
            pltpu.VMEM((sizes[a], part, columns), jnp.float32),
        ]
    sems = pltpu.SemaphoreType.DMA((len(pieces), 3, max(sizes)))
    return pl.pallas_call(
        functools.partial(reduce_kernel, sizes, pieces),
        out_shape=jax.ShapeDtypeStruct((rows, columns), jnp.float32),
        in_specs=[pl.BlockSpec(memory_space=pltpu.VMEM)],
        out_specs=pl.BlockSpec(memory_space=pltpu.VMEM),
        scratch_shapes=landing + sums + [sems, sems],
        compiler_params=pltpu.CompilerParams(
            collective_id=number, has_side_effects=True, vmem_limit_bytes=40 * 2**20
        ),
        name=f"reduce_{number}",
    )(x.reshape(sizes + (rows, columns)))


def dot_first(left, right):
    return lax.dot_general(
        left, right, (((0,), (0,)), ((), ())), precision=HIGHEST, preferred_element_type=jnp.float32
    )


def inverse_kernel(size, width, g_ref, x_ref, a_ref, d_ref):
    eye = lax.broadcasted_iota(jnp.int32, (size, size), 0) == lax.broadcasted_iota(
        jnp.int32, (size, size), 1
    )
    gram = g_ref[...]
    trace = jnp.sum(jnp.where(eye, gram, 0.0), keepdims=True)
    a_ref[...] = gram + jnp.where(eye, 0.0001 * trace / size, 0.0)
    x_ref[...] = jnp.where(eye, 1.0, 0.0)
    strip = lax.broadcasted_iota(jnp.int32, (8, width), 0)
    lane = lax.broadcasted_iota(jnp.int32, (8, width), 1)
    small_eye = jnp.where(
        lax.broadcasted_iota(jnp.int32, (width, width), 0)
        == lax.broadcasted_iota(jnp.int32, (width, width), 1),
        1.0,
        0.0,
    )

    def group(g, _):
        first = pl.multiple_of(g * 8, 8)
        left = d_ref[pl.ds(first, 8), :width]
        right = d_ref[pl.ds(first, 8), width:]
        turned = pltpu.roll(left, lax.rem(width - first, width), 1)
        columns = [jnp.broadcast_to(turned[:, j : j + 1], (8, width)) for j in range(8)]
        for j in range(8):
            scale = lax.rsqrt(columns[j][j : j + 1, :])
            factor = columns[j] * scale
            for m in range(j + 1, 8):
                columns[m] = columns[m] - factor * factor[m : m + 1, :]
            row_left, row_right = left[j : j + 1, :] * scale, right[j : j + 1, :] * scale
            below, here = strip > j, strip == j
            left = jnp.where(here, row_left, jnp.where(below, left - factor * row_left, left))
            right = jnp.where(here, row_right, jnp.where(below, right - factor * row_right, right))
        later = jnp.where(lane >= first + 8, left, 0.0)
        both = jnp.concatenate([left, right], axis=1)
        d_ref[pl.ds(first, 8), :] = both
        d_ref[...] = d_ref[...] - dot_first(later, both)
        return 0

    for k in range(size // width):
        top, end = k * width, (k + 1) * width
        d_ref[:, :width] = a_ref[top:end, top:end]
        d_ref[:, width:] = small_eye
        lax.fori_loop(0, width // 8, group, 0)
        corner = d_ref[:, width:]
        done = jnp.dot(corner, x_ref[top:end, :end], precision=HIGHEST)
        x_ref[top:end, :end] = done
        if end < size:
            panel = jnp.dot(corner, a_ref[top:end, end:], precision=HIGHEST)
            a_ref[end:, end:] = a_ref[end:, end:] - dot_first(panel, panel)
            x_ref[end:, :end] = x_ref[end:, :end] - dot_first(panel, done)


def lower_inverse(gram_total):
    size = gram_total.shape[0]
    width = 128
    return pl.pallas_call(
        functools.partial(inverse_kernel, size, width),
        out_shape=jax.ShapeDtypeStruct((size, size), jnp.float32),
        in_specs=[pl.BlockSpec(memory_space=pltpu.VMEM)],
        out_specs=pl.BlockSpec(memory_space=pltpu.VMEM),
        scratch_shapes=[
            pltpu.VMEM((size, size), jnp.float32),
            pltpu.VMEM((width, 2 * width), jnp.float32),
        ],
        compiler_params=pltpu.CompilerParams(vmem_limit_bytes=24 * 2**20),
        name="lower_inverse",
    )(gram_total)


def per_device(sizes, momentum, grad, q_basis):
    own_rows = momentum.shape[0]
    basis_rows, rank = q_basis.shape
    devices = math.prod(sizes)
    features = basis_rows * devices
    blended = momentum + grad.astype(jnp.float32)
    blended_low = blended.astype(jnp.bfloat16)
    basis = gather(q_basis.astype(jnp.bfloat16), sizes, 0)
    projected = jnp.dot(blended_low, basis, preferred_element_type=jnp.float32)
    local_gram = jnp.dot(projected.T, projected, precision=HIGHEST)
    gram_total = gather(reduce_scatter(local_gram, sizes, 1), sizes, 2)
    inverse = lower_inverse(gram_total)
    orthonormal = jnp.dot(projected, inverse.T, precision=HIGHEST)
    ortho_low = orthonormal.astype(jnp.bfloat16)
    terms = jnp.dot(blended_low.T, ortho_low, preferred_element_type=jnp.float32)
    summed = reduce_scatter(terms.astype(jnp.bfloat16), sizes, 3)
    summed_low = gather(summed.astype(jnp.bfloat16), sizes, 4)
    wide = summed_low.astype(jnp.float32)
    column_rms = jnp.sqrt(jnp.mean(wide * wide, axis=0) + epsilon)
    q_next = summed / column_rms
    stacked = jnp.concatenate(
        [ortho_low, (orthonormal / column_rms).astype(jnp.bfloat16)], axis=0
    )
    result = jnp.dot(stacked, summed_low.T, preferred_element_type=jnp.float32)
    total_rows = own_rows * devices
    momentum_next = blended - (1.0 - damping) * result[:own_rows]
    update = (math.sqrt(total_rows * features / rank) * result[own_rows:]).astype(jnp.bfloat16)
    return (momentum_next, update, q_next)


def solution(mesh):
    spec = P(("mat", "fsdp"), None)
    return jax.shard_map(
        functools.partial(per_device, grid_of(mesh)),
        mesh=mesh,
        in_specs=(spec, spec, spec),
        out_specs=(spec, spec, spec),
        check_vma=False,
    )
```

time: 586 us -> 249 us (0.42)
  waiting for transfers between devices: 357 us -> 0 us
  Pallas kernels: 0 us -> 227 us
  other arithmetic: 137 us -> 8.96 us
  matrix products: 52.4 us -> 8.6 us
  between operations: 18 us -> 0.76 us
  local copies, waits for them, and re-layouts: 16.9 us -> 0.01 us
    psum x1 -> x0, waiting for transfers between devices: 276 us -> none  [per_device(): summed, gram_total = lax.psum((partial_sum, local_gram), 'fsdp')]
    pallas_call x0 -> x6, Pallas kernels: none -> 227 us  [the longest x3 119 us: gather(): pl.pallas_call(functools.partial(gather_kernel, sizes, pieces), out_shape...]
    another operation x17 -> x0, other arithmetic: 120 us -> none  [the longest x14 78.7 us: lower_inverse(): factor_lower = jnp.linalg.cholesky(gram_total + ridge_term * identity)]
    all_gather x1 -> x0, waiting for transfers between devices: 80.6 us -> none  [per_device(): lax.all_gather(basis_low, 'fsdp', axis=0, tiled=True)]
    dot_general x6 -> x5, matrix products: 41 us -> 8.6 us  [the longest x1 2.83 us: per_device(): projected = jnp.dot(blended_low, basis, preferred_element_type=jnp.float32)]
    another operation x34 -> x0, local copies, waits for them, and re-layouts: 14.7 us -> none
    another operation x13 -> x0, matrix products: 11.4 us -> none  [the longest x7 7.34 us: lower_inverse(): lax.linalg.triangular_solve(factor_lower, identity, left_side=True, lower...]
  transfers between devices with their start and end apart: 2 -> 0, of which waited for: 2 -> 0; matrix products, arithmetic and copies ran while one was open for 0% -> 0% of each run, Pallas kernels for 0% -> 0%
where the time goes in v1:
time: 249 us; the launch traced here: 245 us
  Pallas kernels  227 us (91%)
  other arithmetic  8.96 us (4%)
  matrix products  8.6 us (3%)
    pallas_call x3, Pallas kernels, gather(): pl.pallas_call(functools.partial(gather_kernel, sizes, pieces), out_shape...  119 us
    pallas_call x2, Pallas kernels, reduce_scatter(): pl.pallas_call(functools.partial(reduce_kernel, sizes, pieces), out_shape...  70.5 us
    pallas_call x1, Pallas kernels, lower_inverse(): pl.pallas_call(functools.partial(inverse_kernel, size, width), out_shape=...  37.5 us
    convert_element_type x1, other arithmetic, per_device(): (math.sqrt(total_rows * features / rank) * result[own_rows:]).astype(jnp....  5.83 us

profile of v1, /device:TPU:0, one launch (start us, length us, event | category | flops | bytes accessed | tf_op | source)
XLA Modules:
  0.0 244.8 jit_solution(6714658033622623841)
XLA Ops:
  0.6 0.0 copy-start
  0.6 1.2 convert_element_type.30.x_ref
  1.9 50.9 %gather_0.1 = bf16[4,2,2,256,512]{4,3,2,1,0:T(8,128)(2,1)S(1)} custom-call(bf16[256,512]{1,0:T(8,128)(2,1)S(1)} %convert_element_type.30.x_ref), custom_call_target="tpu_custom_call" | custom-call | tf_op jit(solution)/shard_map/gather_0/pallas_call | solution.py:136
  52.8 0.0 copy-done
  52.8 2.8 %fusion.9 = f32[256,512]{1,0:T(8,128)S(1)} fusion(bf16[4096,512]{1,0:T(8,128)(2,1)S(1)} %bitcast.14, f32[256,4096]{1,0:T(8,128)S(1)} %copy-done, bf16[256,4096]{1,0:T(8,128)(2,1)} %param.4), kind=kOutput, calls=%fused_computation.16 | convolution fusion | flops 1076887552 | bytes 11010048 | tf_op jit(solution)/shard_map/dot_general | solution.py:347
  55.6 0.0 copy-start.1
  55.6 1.0 fusion.12
  56.7 24.0 %reduce_1.1.x_ref = f32[32,512]{1,0:T(8,128)S(1)} custom-call(f32[4,2,2,32,512]{4,3,2,1,0:T(8,128)S(1)} %bitcast.16), custom_call_target="tpu_custom_call" | custom-call | tf_op jit(solution)/shard_map/reduce_1/pallas_call | solution.py:251
  80.7 19.3 %gather_2.1 = f32[4,2,2,32,512]{4,3,2,1,0:T(8,128)S(1)} custom-call(f32[32,512]{1,0:T(8,128)S(1)} %reduce_1.1.x_ref), custom_call_target="tpu_custom_call" | custom-call | tf_op jit(solution)/shard_map/gather_2/pallas_call | solution.py:136
  100.1 37.5 %lower_inverse.1 = f32[512,512]{1,0:T(8,128)S(1)} custom-call(f32[512,512]{1,0:T(8,128)S(1)} %bitcast.15), custom_call_target="tpu_custom_call" | custom-call | tf_op jit(solution)/shard_map/lower_inverse/pallas_call | solution.py:325
  137.6 1.1 fusion.11
  138.6 0.0 copy-done.1
  138.6 1.3 convolution_convert_fusion
  140.0 46.4 %reduce_3.1 = f32[256,512]{1,0:T(8,128)S(1)} custom-call(bf16[4,2,2,256,512]{4,3,2,1,0:T(8,128)(2,1)S(1)} %bitcast.13), custom_call_target="tpu_custom_call" | custom-call | tf_op jit(solution)/shard_map/reduce_3/pallas_call | solution.py:251
  186.4 48.3 %gather_4.1 = bf16[4,2,2,256,512]{4,3,2,1,0:T(8,128)(2,1)S(1)} custom-call(bf16[256,512]{1,0:T(8,128)(2,1)S(1)} %convert_element_type.33.x_ref), custom_call_target="tpu_custom_call" | custom-call | tf_op jit(solution)/shard_map/gather_4/pallas_call | solution.py:136
  234.8 1.0 multiply_reduce_fusion
  235.7 0.9 broadcast_divide_fusion
  236.6 2.4 fusion.3
  239.0 5.8 %fusion = (bf16[256,4096]{1,0:T(8,128)(2,1)}, f32[256,4096]{1,0:T(8,128)}) fusion(f32[512,4096]{1,0:T(8,128)S(1)} %fusion.3, f32[256,4096]{1,0:T(8,128)S(1)} %copy-done, bf16[256,4096]{1,0:T(8,128)(2,1)} %param.4), kind=kLoop, calls=%fused_computation.3 | loop fusion | flops 6291456 | bytes 20971520 | tf_op jit(solution)/shard_map/convert_element_type | solution.py:365
  (2 shorter events, 0.0 us)
Async XLA Ops:
  0.6 52.2 %copy-start = (f32[256,4096]{1,0:T(8,128)S(1)}, f32[256,4096]{1,0:T(8,128)}, u32[]{:S(2)}) copy-start(f32[256,4096]{1,0:T(8,128)} %param.3) | copy-start | bytes 12582916
  55.6 83.0 %copy-start.1 = (bf16[256,4096]{1,0:T(8,128)(2,1)S(1)}, bf16[256,4096]{1,0:T(8,128)(2,1)}, u32[]{:S(2)}) copy-start(bf16[256,4096]{1,0:T(8,128)(2,1)} %param.4) | copy-start | bytes 6291460

commit v2 on v1

--- a/solution.py
+++ b/solution.py
@@ -36,21 +36,26 @@
 
 def cut(rows, unit, sizes):
     units = rows // unit
-    side = (units * 3 + 4) // 8
-    counts = [side, side, units - 2 * side]
     long_axis = max(range(3), key=lambda d: sizes[d])
-    others = [d for d in range(3) if d != long_axis]
-    orders = [
-        (long_axis, others[0], others[1]),
-        (others[1], long_axis, others[0]),
-        (others[0], others[1], long_axis),
-    ]
+    first, second = [d for d in range(3) if d != long_axis]
+    tail = units // 8
+    pairs = 2 if units >= 8 else 1
+    share, extra = divmod(units - tail, 2 * pairs)
+    plan = [(tail, (first, second, long_axis), 0)]
+    for k in range(2 * pairs):
+        short = (first, second) if k % 2 == 0 else (second, first)
+        plan.append((share + (k < extra), (long_axis,) + short, k // 2))
     pieces, start = [], 0
-    for count, order in zip(counts, orders):
+    for count, order, wave in plan:
         if count:
-            pieces.append((start, count * unit, order))
+            pieces.append((start, count * unit, order, wave))
         start += count * unit
     return pieces
+
+
+def wavefront(pieces, phases):
+    steps = [(piece[3] + phase, phase, p) for p, piece in enumerate(pieces) for phase in range(phases)]
+    return [(phase, p) for _, phase, p in sorted(steps)]
 
 
 def position(sizes):
@@ -88,7 +93,7 @@
     greet(mine, sizes)
 
     def block(piece, phase, coordinate):
-        start, rows, order = piece
+        start, rows, order, _ = piece
         index = list(mine)
         index[order[phase]] = coordinate
         for d in order[:phase]:
@@ -96,29 +101,31 @@
         return o_ref.at[index[0], index[1], index[2], pl.ds(start, rows)]
 
     sent = []
-    for phase in range(3):
-        if phase == 1:
-            own.wait()
-        for p, piece in enumerate(pieces):
-            if phase:
-                d = piece[2][phase - 1]
-                for off in range(1, sizes[d]):
-                    landed = block(piece, phase - 1, shifted(mine, sizes, d, sizes[d] - off))
-                    pltpu.make_async_copy(landed, landed, recv_sem.at[p, phase - 1, off]).wait()
-            d = piece[2][phase]
+    own_here = False
+    for phase, p in wavefront(pieces, 3):
+        piece = pieces[p]
+        if phase:
+            if not own_here:
+                own.wait()
+                own_here = True
+            d = piece[2][phase - 1]
             for off in range(1, sizes[d]):
-                target = block(piece, phase, mine[d])
-                source = x_ref.at[pl.ds(piece[0], piece[1])] if phase == 0 else target
-                copy = pltpu.make_async_remote_copy(
-                    src_ref=source,
-                    dst_ref=target,
-                    send_sem=send_sem.at[p, phase, off],
-                    recv_sem=recv_sem.at[p, phase, off],
-                    device_id=device_at(mine, sizes, d, shifted(mine, sizes, d, off)),
-                    device_id_type=MESH,
-                )
-                copy.start()
-                sent.append(copy)
+                landed = block(piece, phase - 1, shifted(mine, sizes, d, sizes[d] - off))
+                pltpu.make_async_copy(landed, landed, recv_sem.at[p, phase - 1, off]).wait()
+        d = piece[2][phase]
+        for off in range(1, sizes[d]):
+            target = block(piece, phase, mine[d])
+            source = x_ref.at[pl.ds(piece[0], piece[1])] if phase == 0 else target
+            copy = pltpu.make_async_remote_copy(
+                src_ref=source,
+                dst_ref=target,
+                send_sem=send_sem.at[p, phase, off],
+                recv_sem=recv_sem.at[p, phase, off],
+                device_id=device_at(mine, sizes, d, shifted(mine, sizes, d, off)),
+                device_id_type=MESH,
+            )
+            copy.start()
+            sent.append(copy)
     for p, piece in enumerate(pieces):
         d = piece[2][2]
         for off in range(1, sizes[d]):
@@ -173,14 +180,14 @@
             here = landing[3 * p + phase].at[off - 1]
             pltpu.make_async_copy(here, here, recv_sem.at[p, phase, off]).wait()
 
-    for p, (start, rows, order) in enumerate(pieces):
+    def begin(p, start, rows, order):
         d = order[2]
         for off in range(1, sizes[d]):
             index = [slice(None)] * 3
             index[d] = shifted(mine, sizes, d, off)
             send(p, 0, d, off, x_ref.at[index[0], index[1], index[2], pl.ds(start, rows)])
 
-    for p, (start, rows, order) in enumerate(pieces):
+    def first_sums(p, start, rows, order):
         a, b, c = order
         arrive(p, 0, c)
         low, high = min(a, b), max(a, b)
@@ -203,7 +210,7 @@
         for off in range(1, sizes[b]):
             send(p, 1, b, off, sums[2 * p].at[off - 1])
 
-    for p, (start, rows, order) in enumerate(pieces):
+    def second_sums(p, start, rows, order):
         a, b, c = order
         arrive(p, 1, b)
         for off in list(range(1, sizes[a])) + [0]:
@@ -218,13 +225,17 @@
         for off in range(1, sizes[a]):
             send(p, 2, a, off, landing[3 * p + 2].at[sizes[a] - 1 + off - 1])
 
-    for p, (start, rows, order) in enumerate(pieces):
+    def last_sums(p, start, rows, order):
         a = order[0]
         arrive(p, 2, a)
         total = sums[2 * p + 1][mine[a]]
         for k in range(sizes[a] - 1):
             total += landing[3 * p + 2][k].astype(jnp.float32)
         o_ref[pl.ds(start, rows)] = total
+
+    stages = (begin, first_sums, second_sums, last_sums)
+    for phase, p in wavefront(pieces, 4):
+        stages[phase](p, *pieces[p][:3])
     for copy in sent:
         copy.wait_send()
 
@@ -235,7 +246,7 @@
     unit = 8 if x.dtype == jnp.float32 else 16
     pieces = cut(rows, unit, sizes)
     landing, sums = [], []
-    for _, part, (a, b, c) in pieces:
+    for _, part, (a, b, c), _ in pieces:
         low, high = min(a, b), max(a, b)
         many = lambda k: max(k, 1)
         landing += [
@@ -267,6 +278,23 @@
     )
 
 
+def three(x):
+    high = x.astype(jnp.bfloat16).astype(jnp.float32)
+    rest = x - high
+    middle = rest.astype(jnp.bfloat16).astype(jnp.float32)
+    return high, middle, rest - middle
+
+
+def short_dot(left, right):
+    h, m, l = three(left)
+    lefts = jnp.concatenate([h, h, m, m, h, l], axis=0).astype(jnp.bfloat16)
+    h, m, l = three(right)
+    rights = jnp.concatenate([h, m, h, m, l, h], axis=0).astype(jnp.bfloat16)
+    return lax.dot_general(
+        lefts, rights, (((0,), (0,)), ((), ())), preferred_element_type=jnp.float32
+    )
+
+
 def inverse_kernel(size, width, g_ref, x_ref, a_ref, d_ref):
     eye = lax.broadcasted_iota(jnp.int32, (size, size), 0) == lax.broadcasted_iota(
         jnp.int32, (size, size), 1
@@ -302,7 +330,7 @@
         later = jnp.where(lane >= first + 8, left, 0.0)
         both = jnp.concatenate([left, right], axis=1)
         d_ref[pl.ds(first, 8), :] = both
-        d_ref[...] = d_ref[...] - dot_first(later, both)
+        d_ref[...] = d_ref[...] - short_dot(later, both)
         return 0
 
     for k in range(size // width):

time: 249 us -> 224 us (0.90)
  Pallas kernels: 227 us -> 202 us
    pallas_call x3, Pallas kernels: 119 us -> 105 us  [gather(): pl.pallas_call(functools.partial(gather_kernel, sizes, pieces), out_shape...]
    pallas_call x1, Pallas kernels: 37.5 us -> 30.7 us  [lower_inverse(): pl.pallas_call(functools.partial(inverse_kernel, size, width), out_shape=...]
    pallas_call x2, Pallas kernels: 70.5 us -> 67 us  [reduce_scatter(): pl.pallas_call(functools.partial(reduce_kernel, sizes, pieces), out_shape...]
where the time goes in v2:
time: 224 us; the launch traced here: 221 us
  Pallas kernels  202 us (90%)
  other arithmetic  8.96 us (4%)
  matrix products  8.6 us (4%)
    pallas_call x3, Pallas kernels, gather(): pl.pallas_call(functools.partial(gather_kernel, sizes, pieces), out_shape...  105 us
    pallas_call x2, Pallas kernels, reduce_scatter(): pl.pallas_call(functools.partial(reduce_kernel, sizes, pieces), out_shape...  67 us
    pallas_call x1, Pallas kernels, lower_inverse(): pl.pallas_call(functools.partial(inverse_kernel, size, width), out_shape=...  30.7 us
    convert_element_type x1, other arithmetic, per_device(): (math.sqrt(total_rows * features / rank) * result[own_rows:]).astype(jnp....  5.83 us

profile of v2, /device:TPU:0, one launch (start us, length us, event | category | flops | bytes accessed | tf_op | source)
XLA Modules:
  0.0 220.7 jit_solution(11925746592079891714)
XLA Ops:
  0.6 0.0 copy-start
  0.6 1.2 convert_element_type.30.x_ref
  1.9 51.4 %gather_0.1 = bf16[4,2,2,256,512]{4,3,2,1,0:T(8,128)(2,1)S(1)} custom-call(bf16[256,512]{1,0:T(8,128)(2,1)S(1)} %convert_element_type.30.x_ref), custom_call_target="tpu_custom_call" | custom-call | tf_op jit(solution)/shard_map/gather_0/pallas_call | solution.py:143
  53.2 0.0 copy-done
  53.2 2.8 %fusion.9 = f32[256,512]{1,0:T(8,128)S(1)} fusion(bf16[4096,512]{1,0:T(8,128)(2,1)S(1)} %bitcast.14, f32[256,4096]{1,0:T(8,128)S(1)} %copy-done, bf16[256,4096]{1,0:T(8,128)(2,1)} %param.4), kind=kOutput, calls=%fused_computation.16 | convolution fusion | flops 1076887552 | bytes 11010048 | tf_op jit(solution)/shard_map/dot_general | solution.py:375
  56.1 0.0 copy-start.1
  56.1 1.0 fusion.12
  57.1 20.3 %reduce_1.1.x_ref = f32[32,512]{1,0:T(8,128)S(1)} custom-call(f32[4,2,2,32,512]{4,3,2,1,0:T(8,128)S(1)} %bitcast.16), custom_call_target="tpu_custom_call" | custom-call | tf_op jit(solution)/shard_map/reduce_1/pallas_call | solution.py:262
  77.4 18.8 %gather_2.1 = f32[4,2,2,32,512]{4,3,2,1,0:T(8,128)S(1)} custom-call(f32[32,512]{1,0:T(8,128)S(1)} %reduce_1.1.x_ref), custom_call_target="tpu_custom_call" | custom-call | tf_op jit(solution)/shard_map/gather_2/pallas_call | solution.py:143
  96.2 30.7 %lower_inverse.1 = f32[512,512]{1,0:T(8,128)S(1)} custom-call(f32[512,512]{1,0:T(8,128)S(1)} %bitcast.15), custom_call_target="tpu_custom_call" | custom-call | tf_op jit(solution)/shard_map/lower_inverse/pallas_call | solution.py:353
  126.9 1.1 fusion.11
  128.0 0.0 copy-done.1
  128.0 1.3 convolution_convert_fusion
  129.3 46.7 %reduce_3.1 = f32[256,512]{1,0:T(8,128)S(1)} custom-call(bf16[4,2,2,256,512]{4,3,2,1,0:T(8,128)(2,1)S(1)} %bitcast.13), custom_call_target="tpu_custom_call" | custom-call | tf_op jit(solution)/shard_map/reduce_3/pallas_call | solution.py:262
  176.0 34.6 %gather_4.1 = bf16[4,2,2,256,512]{4,3,2,1,0:T(8,128)(2,1)S(1)} custom-call(bf16[256,512]{1,0:T(8,128)(2,1)S(1)} %convert_element_type.33.x_ref), custom_call_target="tpu_custom_call" | custom-call | tf_op jit(solution)/shard_map/gather_4/pallas_call | solution.py:143
  210.6 1.0 multiply_reduce_fusion
  211.6 0.9 broadcast_divide_fusion
  212.5 2.4 %fusion.3 = f32[512,4096]{1,0:T(8,128)S(1)} fusion(bf16[4096,512]{1,0:T(8,128)(2,1)S(1)} %bitcast.12, bf16[256,512]{1,0:T(8,128)(2,1)S(1)} %get-tuple-element.6, bf16[256,512]{1,0:T(8,128)(2,1)S(1)} %get-tuple-element.7), kind=kOutput, calls=%fused_computation.8 | convolution fusion | flops 2148532224 | bytes 13107200 | tf_op jit(solution)/shard_map/dot_general | solution.py:390
  214.9 5.8 %fusion = (bf16[256,4096]{1,0:T(8,128)(2,1)}, f32[256,4096]{1,0:T(8,128)}) fusion(f32[512,4096]{1,0:T(8,128)S(1)} %fusion.3, f32[256,4096]{1,0:T(8,128)S(1)} %copy-done, bf16[256,4096]{1,0:T(8,128)(2,1)} %param.4), kind=kLoop, calls=%fused_computation.3 | loop fusion | flops 6291456 | bytes 20971520 | tf_op jit(solution)/shard_map/convert_element_type | solution.py:393
  (2 shorter events, 0.0 us)
Async XLA Ops:
  0.6 52.6 %copy-start = (f32[256,4096]{1,0:T(8,128)S(1)}, f32[256,4096]{1,0:T(8,128)}, u32[]{:S(2)}) copy-start(f32[256,4096]{1,0:T(8,128)} %param.3) | copy-start | bytes 12582916
  56.1 71.9 %copy-start.1 = (bf16[256,4096]{1,0:T(8,128)(2,1)S(1)}, bf16[256,4096]{1,0:T(8,128)(2,1)}, u32[]{:S(2)}) copy-start(bf16[256,4096]{1,0:T(8,128)(2,1)} %param.4) | copy-start | bytes 6291460
